TPU v7x, 32 devices: a whole 2x2x4 slice. The times are simulated.
32 devices in a mesh: ty: 4 (over y, x), tx: 8 (over z, core).
Axes of the slice: x: 2, y: 2, z: 4, core: 2. Of those that a mesh axis runs over, the one named last changes fastest.
Arguments:
- surface_levels: float32 [512, 16384], P('ty', 'tx'), may hold values from -6 to 6
- bearing_index: int32 [4], replicated, may hold values from 0 to 15
- stencil_displacements: int32 [4], replicated, may hold values from -4 to 4
- camera_altitude_class: int32 [4], replicated, may hold values from 0 to 3
Outputs:
- margin: float32 [4, 512, 16384], P(None, 'ty', 'tx')
Inputs may be any that keep to these rules, and one draw needn't show every extreme that they name: `bearing_index`: azimuth indices.
All inputs are finite; a program needn't handle non-finite values.
Results may differ from a plain program's by a relative error of at most 0.00002.
Values sent between devices are 32-bit elements; how exact they have to be, the bound alone decides.
A program may use at most 192 MiB of HBM per device.

v0:
```python
import math

import jax
import jax.numpy as jnp
from jax import lax
from jax.sharding import PartitionSpec as P

AZIMUTHS = 4
STENCIL_REACH = 4


def padded(cells, sides, width):
    for axis, dim in sides:
        count = lax.axis_size(axis)
        ends = count - 1
        head = lax.slice_in_dim(cells, 0, width, axis=dim)
        tail = lax.slice_in_dim(cells, cells.shape[dim] - width, cells.shape[dim], axis=dim)
        cells = jnp.concatenate(
            [
                lax.ppermute(tail, axis, [(i, (i + 1) % count) for i in range(ends)]),
                cells,
                lax.ppermute(head, axis, [((i + 1) % count, i) for i in range(ends)]),
            ],
            axis=dim,
        )
    return cells


def prefix(part, axis, combine, identity):
    place = lax.axis_index(axis)
    gathered = lax.all_gather(part, axis)
    state = jnp.zeros_like(part) + jnp.asarray(identity, part.dtype)

    def one(hop, state):
        return combine(state, lax.dynamic_index_in_dim(gathered, hop, 0, False))

    return lax.fori_loop(0, place, one, state)


def view_tables(bearing_index, camera_altitude_class, easting_span):
    angle_idx = bearing_index.astype(jnp.float32)
    frac = ((bearing_index * 5 % 16).astype(jnp.float32) + 0.5) / 16.0
    theta = (angle_idx - 7.5) * (math.pi / 32.0)
    stride = 1.0 / jnp.cos(theta)
    slope = (1.0 + camera_altitude_class.astype(jnp.float32)) / (4.0 * easting_span)
    cube = frac * frac * frac
    square = frac * frac
    weights = jnp.stack(
        [
            (-cube + 2.0 * square - frac) / 2.0,
            (3.0 * cube - 5.0 * square + 2.0) / 2.0,
            (-3.0 * cube + 4.0 * square + frac) / 2.0,
            (cube - square) / 2.0,
        ],
        axis=1,
    )
    return (weights, stride * slope)


def on_device(surface_levels, bearing_index, stencil_displacements, camera_altitude_class):
    northing_extent, easting_extent = surface_levels.shape
    easting_span = easting_extent * lax.axis_size("tx")
    weights, rise = view_tables(bearing_index, camera_altitude_class, easting_span)
    bordered_surface = padded(surface_levels, (("ty", 0),), STENCIL_REACH + 2)
    first_col = lax.axis_index("tx") * easting_extent
    columns = (first_col + jnp.arange(easting_extent)).astype(jnp.float32)
    stacked = []
    for which in range(AZIMUTHS):
        strips = jnp.zeros((northing_extent, easting_extent), jnp.float32)
        for tap_index in range(4):
            start = stencil_displacements[which] + tap_index + STENCIL_REACH + 1
            strips = strips + weights[which, tap_index] * lax.dynamic_slice_in_dim(
                bordered_surface, start, northing_extent, 0
            )
        stacked.append(strips + rise[which] * columns[None, :])
    lifted = jnp.stack(stacked, axis=0)
    running = lax.cummax(lifted, axis=2)
    row_peak = running[:, :, -1]
    before = prefix(row_peak, "tx", jnp.maximum, jnp.full_like(row_peak, -jnp.inf))
    lowest = jnp.full((AZIMUTHS, northing_extent, 1), -jnp.inf, jnp.float32)
    earlier = jnp.concatenate([lowest, running[:, :, :-1]], axis=2)
    horizon = jnp.maximum(earlier, before[:, :, None])
    margin = jnp.maximum(horizon - lifted, 0.0)
    return margin


def solution(mesh):
    return jax.shard_map(
        on_device,
        mesh=mesh,
        in_specs=(P("ty", "tx"), P(), P(), P()),
        out_specs=P(None, "ty", "tx"),
        check_vma=False,
    )
```

profile of v0, /device:TPU:13, one launch (start us, length us, event | category | flops | bytes accessed | tf_op | source)
XLA Modules:
  0.0 88.7 jit_solution(15927352842759465589)
XLA Ops:
  0.0 0.9 fusion.15
  0.9 3.1 %collective-permute-start = (f32[6,2048]{1,0:T(8,128)S(1)}, f32[6,2048]{1,0:T(8,128)S(1)}, u32[]{:S(2)}, u32[]{:S(2)}) collective-permute-start(f32[6,2048]{1,0:T(8,128)S(1)} %get-tuple-element.43), channel_id=1, source_target_pairs={{0,8},{8,16},{16,24},{1,9},{9,17},{17,25},{2,10},{10,18},{18,26},{... | collective-permute-start | bytes 147464 | tf_op jit(solution)/shard_map/ppermute | solution.py:20
  4.0 3.1 %collective-permute-start.1 = (f32[6,2048]{1,0:T(8,128)S(1)}, f32[6,2048]{1,0:T(8,128)S(1)}, u32[]{:S(2)}, u32[]{:S(2)}) collective-permute-start(f32[6,2048]{1,0:T(8,128)S(1)} %get-tuple-element.44), channel_id=1, source_target_pairs={{8,0},{16,8},{24,16},{9,1},{17,9},{25,17},{10,2},{18,10},{26,18},{... | collective-permute-start | bytes 147464 | tf_op jit(solution)/shard_map/ppermute | solution.py:22
  7.1 1.5 %fusion.21 = (s32[1]{0:T(128)}, s32[1]{0:T(128)}, s32[1]{0:T(128)}, s32[1]{0:T(128)}) fusion(s32[4]{0:T(128)} %param.8), kind=kLoop, calls=%fused_computation.43 | loop fusion | bytes 32 | tf_op jit(solution)/shard_map/slice | solution.py:71
  8.6 0.8 subtract_multiply_fusion.1
  9.3 0.7 fusion.16
  10.0 0.6 convert_multiply_fusion.1
  10.7 0.6 convert_multiply_fusion.3
  11.2 0.6 fusion.19
  11.8 0.6 convert_multiply_fusion
  12.5 0.7 fusion.17
  13.2 0.6 convert_multiply_fusion.2
  24.5 1.6 %copy.19 = f32[128,2048]{0,1:T(8,128)S(1)} copy(f32[128,2048]{1,0:T(8,128)} %param.6) | data formatting | bytes 2097152 | tf_op args[0]
  36.1 0.0 collective-permute-done
  36.1 0.4 copy.18
  36.5 0.0 collective-permute-done.1
  36.5 0.4 copy.20
  36.9 0.9 pad_maximum_fusion
  37.8 8.0 %add_add_fusion.3 = (f32[128,2048]{0,1:T(8,128)S(1)}, f32[128,2048]{0,1:T(8,128)S(1)}) fusion(f32[140,2048]{0,1:T(8,128)S(1)} %pad_maximum_fusion, s32[]{:T(128)S(6)} %select_n.63, s32[]{:T(128)S(6)} %select_n.62, s32[]{:T(128)S(6)} %select_n.61, s32[]{:T(128)S(6)} %select_n.60, f32[2048]{0:T(1024)S(1)} %convert_multiply_fusion.3, f32[]{:T(128)} %bitcast.10, ...), kind=kLoop, calls=%fused_computation.16 | loop fusion | flops 4194304 | bytes 10502208 | tf_op jit(solution)/shard_map/add | solution.py:75
  45.7 0.6 copy.21
  46.3 0.6 copy.23
  47.0 8.0 %add_add_fusion.2 = (f32[128,2048]{0,1:T(8,128)S(1)}, f32[128,2048]{0,1:T(8,128)S(1)}) fusion(f32[140,2048]{0,1:T(8,128)S(1)} %pad_maximum_fusion, s32[]{:T(128)S(6)} %select_n.67, s32[]{:T(128)S(6)} %select_n.66, s32[]{:T(128)S(6)} %select_n.65, s32[]{:T(128)S(6)} %select_n.64, f32[2048]{0:T(1024)S(1)} %convert_multiply_fusion.2, f32[]{:T(128)} %bitcast.24, ...), kind=kLoop, calls=%fused_computation.15 | loop fusion | flops 4194304 | bytes 10502208 | tf_op jit(solution)/shard_map/add | solution.py:75
  54.9 0.0 copy-start.2
  54.9 0.6 copy.22
  55.6 0.3 copy-done.2
  55.9 0.6 copy.24
  56.5 0.3 fusion
  56.8 0.0 copy-start
  56.8 2.0 %copy-done = f32[4,128,16,128]{1,2,3,0:T(8,128)} copy-done((f32[4,128,16,128]{1,2,3,0:T(8,128)}, f32[4,128,16,128]{1,2,3,0:T(8,128)S(1)}, u32[]{:S(2)}) %copy-start) | copy-done | bytes 4194328
  58.9 2.6 %broadcast_maximum_fusion = f32[4,128,16,128]{1,2,3,0:T(8,128)S(1)} fusion(f32[4,128,16,128]{1,2,3,0:T(8,128)} %copy-done, f32[4,128,16]{1,2,0:T(8,128)S(1)} %slice.149), kind=kLoop, calls=%fused_computation.12 | loop fusion | flops 1048576 | bytes 8421376 | tf_op jit(solution)/shard_map/reduce_window_max | solution.py:77
  61.5 1.3 %copy.25 = f32[4,128,16,128]{1,3,2,0:T(8,128)S(1)} copy(f32[4,128,16,128]{1,2,3,0:T(8,128)S(1)} %broadcast_maximum_fusion) | data formatting | bytes 8388608 | tf_op jit(solution)/shard_map/reduce_window_max | solution.py:77
  62.8 0.0 copy-start.1
  62.8 2.0 %copy-done.1 = f32[4,128,16,128]{1,3,2,0:T(8,128)} copy-done((f32[4,128,16,128]{1,3,2,0:T(8,128)}, f32[4,128,16,128]{1,3,2,0:T(8,128)S(1)}, u32[]{:S(2)}) %copy-start.1) | copy-done | bytes 4194328
  64.8 14.1 %all-gather = f32[32,128,1]{1,2,0:T(1,128)S(1)} all-gather(f32[4,128,1]{1,2,0:T(1,128)S(1)} %slice.151), channel_id=2, replica_groups=mesh['ty'=4,'tx'=8] {'tx'}, dimensions={0}, use_global_device_ids=true | all-gather | bytes 18432 | tf_op jit(solution)/shard_map/all_gather | solution.py:31
  78.9 0.1 while.10
  79.0 4.3 %fusion.8 = f32[4,128,2048]{1,2,0:T(8,128)} fusion(f32[1,128,2048]{1,2,0:T(8,128)} %bitcast.78, f32[1,128,2048]{1,2,0:T(8,128)S(1)} %bitcast.74, f32[1,128,2048]{1,2,0:T(8,128)S(1)} %bitcast.76, f32[1,128,2048]{1,2,0:T(8,128)S(1)} %bitcast.72, f32[4,128,2047]{1,2,0:T(8,128)} %bitcast.70, f32[4,128]{1,0:T(4,128)S(1)} %get-tuple-element.28), kind=kLoop, calls=%fused_computation.10 | loop fusion | flops 6291456 | bytes 12582912 | tf_op jit(solution)/shard_map/max | solution.py:83
  83.3 5.3 %copy.26 = f32[4,128,2048]{2,1,0:T(8,128)} copy(f32[4,128,2048]{1,2,0:T(8,128)} %fusion.8) | data formatting | bytes 8388608 | tf_op jit(solution)/shard_map/max | solution.py:83
  (9 shorter events, 0.1 us)
Async XLA Ops:
  0.9 35.2 %collective-permute-start = (f32[6,2048]{1,0:T(8,128)S(1)}, f32[6,2048]{1,0:T(8,128)S(1)}, u32[]{:S(2)}, u32[]{:S(2)}) collective-permute-start(f32[6,2048]{1,0:T(8,128)S(1)} %get-tuple-element.43), channel_id=1, source_target_pairs={{0,8},{8,16},{16,24},{1,9},{9,17},{17,25},{2,10},{10,18},{18,26},{... | collective-permute-start | bytes 147464 | tf_op jit(solution)/shard_map/ppermute | solution.py:20
  4.0 32.5 %collective-permute-start.1 = (f32[6,2048]{1,0:T(8,128)S(1)}, f32[6,2048]{1,0:T(8,128)S(1)}, u32[]{:S(2)}, u32[]{:S(2)}) collective-permute-start(f32[6,2048]{1,0:T(8,128)S(1)} %get-tuple-element.44), channel_id=1, source_target_pairs={{8,0},{16,8},{24,16},{9,1},{17,9},{25,17},{10,2},{18,10},{26,18},{... | collective-permute-start | bytes 147464 | tf_op jit(solution)/shard_map/ppermute | solution.py:22
  54.9 1.0 %copy-start.2 = (f32[128,2048]{0,1:T(8,128)}, f32[128,2048]{0,1:T(8,128)S(1)}, u32[]{:S(2)}) copy-start(f32[128,2048]{0,1:T(8,128)S(1)} %get-tuple-element.42) | copy-start | bytes 3145732
  56.8 2.0 %copy-start = (f32[4,128,16,128]{1,2,3,0:T(8,128)}, f32[4,128,16,128]{1,2,3,0:T(8,128)S(1)}, u32[]{:S(2)}) copy-start(f32[4,128,16,128]{1,2,3,0:T(8,128)S(1)} %fusion) | copy-start | bytes 12582916
  62.8 2.0 %copy-start.1 = (f32[4,128,16,128]{1,3,2,0:T(8,128)}, f32[4,128,16,128]{1,3,2,0:T(8,128)S(1)}, u32[]{:S(2)}) copy-start(f32[4,128,16,128]{1,3,2,0:T(8,128)S(1)} %copy.25) | copy-start | bytes 12582916
where the time goes:
time: 89.5 us; the launch traced here: 88.7 us
  other arithmetic  27.4 us (31%)
  between operations  20.9 us (23%)
  local copies, waits for them, and re-layouts  20 us (22%)
  blocking collectives  14.1 us (16%)
  starting transfers between devices  6.18 us (7%)
    add x2, other arithmetic, on_device(): stacked.append(strips + rise[which] * columns[None, :])  15.9 us
    all_gather x1, blocking collectives, prefix(): gathered = lax.all_gather(part, axis)  14.1 us
    unnamed x7, local copies, waits for them, and re-layouts  5.9 us
    max x1, local copies, waits for them, and re-layouts, on_device(): margin = jnp.maximum(horizon - lifted, 0.0)  5.34 us
    max x1, other arithmetic, on_device(): margin = jnp.maximum(horizon - lifted, 0.0)  4.33 us
    ppermute x1, starting transfers between devices, padded(): lax.ppermute(tail, axis, [(i, (i + 1) % count) for i in range(ends)])  3.12 us
    ppermute x1, starting transfers between devices, padded(): lax.ppermute(head, axis, [((i + 1) % count, i) for i in range(ends)])  3.06 us
    another operation x1, other arithmetic, on_device(): running = lax.cummax(lifted, axis=2)  2.62 us
  transfers between devices with their start and end apart: 2, of which 0 were waited for; matrix products, arithmetic and copies ran while one was open for 10% of the time, Pallas kernels for 0%

commit v1 on v0

v1 whole, which is shorter than its diff:
```python
import functools
import math

import jax
import jax.numpy as jnp
from jax import lax
from jax.experimental import pallas as pl
from jax.experimental.pallas import tpu as pltpu
from jax.sharding import PartitionSpec as P

AZIMUTHS = 4
STENCIL_REACH = 4
LANES = 128
SUB = 8
MESH = pl.DeviceIdType.MESH


def view_rows(bearing, camera, easting_span):
    shape = (SUB, LANES)
    a = jnp.full(shape, bearing, jnp.int32).astype(jnp.float32)
    b = jnp.full(shape, lax.rem(bearing * 5, 16), jnp.int32).astype(jnp.float32)
    cam = jnp.full(shape, camera, jnp.int32).astype(jnp.float32)
    frac = (b + 0.5) / 16.0
    theta = (a - 7.5) * (math.pi / 32.0)
    stride = 1.0 / jnp.cos(theta)
    slope = (1.0 + cam) / (4.0 * easting_span)
    cube = frac * frac * frac
    square = frac * frac
    weights = (
        (-cube + 2.0 * square - frac) / 2.0,
        (3.0 * cube - 5.0 * square + 2.0) / 2.0,
        (-3.0 * cube + 4.0 * square + frac) / 2.0,
        (cube - square) / 2.0,
    )
    return weights, stride * slope


def exchange_kernel(
    bearing_ref, shift_ref, camera_ref, surface_hbm,
    lifted_ref, running_ref, before_ref,
    surf, above, below, edge, peaks, edge_peaks, message, inbox,
    load_sem, up_send, up_recv, down_send, down_recv, peak_send, peak_recv,
):
    rows, cols = surface_hbm.shape
    chunks, tiles = cols // LANES, rows // SUB
    ny, nx = lax.axis_size("ty"), lax.axis_size("tx")
    ty, tx = lax.axis_index("ty"), lax.axis_index("tx")
    barrier = pltpu.get_barrier_semaphore()

    def load(c):
        return pltpu.make_async_copy(
            surface_hbm.at[:, pl.ds(c * LANES, LANES)], surf.at[c], load_sem.at[c]
        )

    for c in range(chunks):
        load(c).start()

    @pl.when(ty > 0)
    def _():
        pl.semaphore_signal(barrier, 1, device_id={"ty": ty - 1}, device_id_type=MESH)

    @pl.when(ty < ny - 1)
    def _():
        pl.semaphore_signal(barrier, 1, device_id={"ty": ty + 1}, device_id_type=MESH)

    for i in range(nx - 1):

        @pl.when(i < tx)
        def _():
            pl.semaphore_signal(barrier, 1, device_id={"tx": i}, device_id_type=MESH)

    weights, rise = [], []
    for k in range(AZIMUTHS):
        w, s = view_rows(bearing_ref[k], camera_ref[k], cols * nx)
        weights.append(w)
        rise.append(s)
    lane = lax.broadcasted_iota(jnp.int32, (SUB, LANES), 1)
    first = (tx * cols + lane).astype(jnp.float32)

    for c in range(chunks):
        load(c).wait()
    sends = jnp.where(ty > 0, 1, 0) + jnp.where(ty < ny - 1, 1, 0) + (nx - 1 - tx)
    pl.semaphore_wait(barrier, sends)

    def to_above():
        return pltpu.make_async_remote_copy(
            surf.at[:, pl.ds(0, SUB), :], below, up_send, up_recv,
            device_id={"ty": ty - 1}, device_id_type=MESH,
        )

    def to_below():
        return pltpu.make_async_remote_copy(
            surf.at[:, pl.ds(rows - SUB, SUB), :], above, down_send, down_recv,
            device_id={"ty": ty + 1}, device_id_type=MESH,
        )

    @pl.when(ty < ny - 1)
    def _():
        to_below().start()

    @pl.when(ty > 0)
    def _():
        to_above().start()

    def stencil(read, row):
        top = [None] * AZIMUTHS
        for c in range(chunks):
            col = first + float(c * LANES)
            for k in range(AZIMUTHS):
                acc = weights[k][0] * read(c, k, 0)
                for j in range(1, 4):
                    acc = acc + weights[k][j] * read(c, k, j)
                acc = acc + rise[k] * col
                lifted_ref[k, c, pl.ds(row, SUB), :] = acc
                top[k] = acc if c == 0 else jnp.maximum(top[k], acc)
        return top

    def inner(t, _):
        row = pl.multiple_of(t * SUB, SUB)
        top = stencil(
            lambda c, k, j: surf[c, pl.ds(row + shift_ref[k] + (j - 1), SUB), :], row
        )
        for k in range(AZIMUTHS):
            peaks[k, pl.ds(row, SUB), :] = top[k]
        return 0

    lowest = jnp.full((SUB, LANES), -jnp.inf, jnp.float32)
    for k in range(AZIMUTHS):
        peaks[k, pl.ds(0, SUB), :] = lowest
        peaks[k, pl.ds(rows - SUB, SUB), :] = lowest
    lax.fori_loop(1, tiles - 1, inner, 0)
    for k in range(AZIMUTHS):
        message[pl.ds(k, 1), :] = jnp.max(peaks[k].T, axis=0, keepdims=True)
    message[pl.ds(AZIMUTHS, SUB - AZIMUTHS), :] = jnp.full(
        (SUB - AZIMUTHS, rows), -jnp.inf, jnp.float32
    )
    before_ref[...] = jnp.full(before_ref.shape, -jnp.inf, jnp.float32)

    @pl.when(ty == 0)
    def _():
        above[...] = jnp.zeros(above.shape, jnp.float32)

    @pl.when(ty == ny - 1)
    def _():
        below[...] = jnp.zeros(below.shape, jnp.float32)

    @pl.when(ty < ny - 1)
    def _():
        to_below().wait_send()
        to_above().wait_recv()

    @pl.when(ty > 0)
    def _():
        to_above().wait_send()
        to_below().wait_recv()

    for c in range(chunks):
        edge[0, c, pl.ds(0, SUB), :] = above[c]
        edge[0, c, pl.ds(SUB, 2 * SUB), :] = surf[c, pl.ds(0, 2 * SUB), :]
        edge[1, c, pl.ds(0, 2 * SUB), :] = surf[c, pl.ds(rows - 2 * SUB, 2 * SUB), :]
        edge[1, c, pl.ds(2 * SUB, SUB), :] = below[c]
    for e in range(2):
        top = stencil(
            lambda c, k, j: edge[e, c, pl.ds(SUB + shift_ref[k] + (j - 1), SUB), :],
            e * (rows - SUB),
        )
        for k in range(AZIMUTHS):
            edge_peaks[pl.ds((2 * k + e) * SUB, SUB), :] = top[k]
    for q in range(2 * AZIMUTHS, LANES // SUB):
        edge_peaks[pl.ds(q * SUB, SUB), :] = lowest
    message[pl.ds(AZIMUTHS, 1), pl.ds(0, LANES)] = jnp.max(
        edge_peaks[...].T, axis=0, keepdims=True
    )

    def to_right(i):
        return pltpu.make_async_remote_copy(
            message, inbox.at[tx], peak_send.at[i], peak_recv.at[tx],
            device_id={"tx": i}, device_id_type=MESH,
        )

    def from_left(i):
        return pltpu.make_async_remote_copy(
            message, inbox.at[i], peak_send.at[i], peak_recv.at[i],
            device_id={"tx": i}, device_id_type=MESH,
        )

    for i in reversed(range(1, nx)):

        @pl.when(i > tx)
        def _():
            to_right(i).start()

    def scan(q, _):
        k = q // tiles
        row = pl.multiple_of((q % tiles) * SUB, SUB)
        carry = None
        for c in range(chunks):
            x = lifted_ref[k, c, pl.ds(row, SUB), :]
            step = 1
            while step < LANES:
                rolled = pltpu.roll(x, step, axis=1)
                x = jnp.maximum(x, jnp.where(lane >= step, rolled, x))
                step *= 2
            last = jnp.broadcast_to(x[:, LANES - 1 :], (SUB, LANES))
            running_ref[k, c, pl.ds(row, SUB), :] = x if c == 0 else jnp.maximum(x, carry)
            carry = last if c == 0 else jnp.maximum(carry, last)
        return 0

    lax.fori_loop(0, AZIMUTHS * tiles, scan, 0)

    for i in range(nx):

        @pl.when(i > tx)
        def _():
            to_right(i).wait_send()

        @pl.when(i < tx)
        def _():
            from_left(i).wait_recv()
            before_ref[...] = jnp.maximum(before_ref[...], inbox[i])


def margin_kernel(lifted_ref, running_ref, before_ref, out_hbm, staged, wide, edge_wide, sem):
    _, chunks, rows, _ = lifted_ref.shape
    tiles = rows // SUB

    def put(k):
        return pltpu.make_async_copy(staged.at[k], out_hbm.at[k], sem.at[k])

    edges = before_ref[pl.ds(AZIMUTHS, 1), pl.ds(0, LANES)]
    edge_wide[...] = jnp.broadcast_to(edges, (LANES, LANES)).T
    for k in range(AZIMUTHS):
        wide[...] = jnp.broadcast_to(before_ref[pl.ds(k, 1), :], (LANES, rows)).T
        wide[pl.ds(0, SUB), :] = edge_wide[pl.ds(2 * k * SUB, SUB), :]
        wide[pl.ds(rows - SUB, SUB), :] = edge_wide[pl.ds((2 * k + 1) * SUB, SUB), :]

        def one(t, _):
            row = pl.multiple_of(t * SUB, SUB)
            bound = wide[pl.ds(row, SUB), :]
            for c in range(chunks):
                high = jnp.maximum(running_ref[k, c, pl.ds(row, SUB), :], bound)
                staged[k, pl.ds(row, SUB), pl.ds(c * LANES, LANES)] = (
                    high - lifted_ref[k, c, pl.ds(row, SUB), :]
                )
            return 0

        lax.fori_loop(0, tiles, one, 0)
        put(k).start()
    for k in range(AZIMUTHS):
        put(k).wait()


def on_device(surface_levels, bearing_index, stencil_displacements, camera_altitude_class):
    rows, cols = surface_levels.shape
    chunks = cols // LANES
    nx = lax.axis_size("tx")
    f32 = jnp.float32
    dma = pltpu.SemaphoreType.DMA
    smem = pl.BlockSpec(memory_space=pltpu.SMEM)
    vmem = pl.BlockSpec(memory_space=pltpu.VMEM)
    hbm = pl.BlockSpec(memory_space=pltpu.HBM)
    block = (AZIMUTHS, chunks, rows, LANES)
    lifted, running, before = pl.pallas_call(
        exchange_kernel,
        out_shape=(pltpu.VMEM(block, f32), pltpu.VMEM(block, f32), pltpu.VMEM((SUB, rows), f32)),
        in_specs=[smem, smem, smem, hbm],
        out_specs=(vmem, vmem, vmem),
        scratch_shapes=[
            pltpu.VMEM((chunks, rows, LANES), f32),
            pltpu.VMEM((chunks, SUB, LANES), f32),
            pltpu.VMEM((chunks, SUB, LANES), f32),
            pltpu.VMEM((2, chunks, 3 * SUB, LANES), f32),
            pltpu.VMEM((AZIMUTHS, rows, LANES), f32),
            pltpu.VMEM((LANES, LANES), f32),
            pltpu.VMEM((SUB, rows), f32),
            pltpu.VMEM((nx, SUB, rows), f32),
            dma((chunks,)),
            dma, dma, dma, dma,
            dma((nx,)),
            dma((nx,)),
        ],
        compiler_params=pltpu.CompilerParams(
            collective_id=0, has_side_effects=True, vmem_limit_bytes=24 * 2**20
        ),
        name="exchange",
    )(bearing_index, stencil_displacements, camera_altitude_class, surface_levels)
    return pl.pallas_call(
        margin_kernel,
        out_shape=jax.ShapeDtypeStruct((AZIMUTHS, rows, cols), f32),
        in_specs=[vmem, vmem, vmem],
        out_specs=hbm,
        scratch_shapes=[
            pltpu.VMEM((AZIMUTHS, rows, cols), f32),
            pltpu.VMEM((rows, LANES), f32),
            pltpu.VMEM((LANES, LANES), f32),
            dma((AZIMUTHS,)),
        ],
        compiler_params=pltpu.CompilerParams(vmem_limit_bytes=24 * 2**20),
        name="margin",
    )(lifted, running, before)


def solution(mesh):
    return jax.shard_map(
        on_device,
        mesh=mesh,
        in_specs=(P("ty", "tx"), P(), P(), P()),
        out_specs=P(None, "ty", "tx"),
        check_vma=False,
    )
```

time: 89.5 us -> 54.5 us (0.61)
  the two profiles are of different devices: /device:TPU:13 before, /device:TPU:0 now
where the time goes in v1:
time: 54.5 us; the launch traced here: 54.3 us
  Pallas kernels  51.1 us (94%)
  local copies, waits for them, and re-layouts  3.19 us (6%)
    pallas_call x1, Pallas kernels, on_device(): pl.pallas_call(exchange_kernel, out_shape=(pltpu.VMEM(block, f32), pltpu....  48.4 us
    unnamed x8, local copies, waits for them, and re-layouts  3.19 us
    pallas_call x1, Pallas kernels, on_device(): pl.pallas_call(margin_kernel, out_shape=jax.ShapeDtypeStruct((AZIMUTHS, r...  2.72 us

profile of v1, /device:TPU:0, one launch (start us, length us, event | category | flops | bytes accessed | tf_op | source)
XLA Modules:
  0.0 54.3 jit_solution(12622148353228247414)
XLA Ops:
  0.0 0.0 copy-start
  0.0 1.2 %copy-done = f32[128,2048]{1,0:T(8,128)S(1)} copy-done((f32[128,2048]{1,0:T(8,128)S(1)}, f32[128,2048]{1,0:T(8,128)}, u32[]{:S(2)}) %copy-start) | copy-done | bytes 1048600
  1.2 0.0 copy-start.1
  1.2 0.7 %copy-done.1 = s32[4]{0:T(128)S(1)} copy-done((s32[4]{0:T(128)S(1)}, s32[4]{0:T(128)}, u32[]{:S(2)}) %copy-start.1) | copy-done | bytes 40
  1.9 0.0 copy-start.2
  1.9 0.7 %copy-done.2 = s32[4]{0:T(128)S(1)} copy-done((s32[4]{0:T(128)S(1)}, s32[4]{0:T(128)}, u32[]{:S(2)}) %copy-start.2) | copy-done | bytes 40
  2.5 0.0 copy-start.3
  2.5 0.7 %copy-done.3 = s32[4]{0:T(128)S(1)} copy-done((s32[4]{0:T(128)S(1)}, s32[4]{0:T(128)}, u32[]{:S(2)}) %copy-start.3) | copy-done | bytes 40
  3.2 48.4 %exchange.1 = (f32[4,16,128,128]{3,2,1,0:T(8,128)S(1)}, f32[4,16,128,128]{3,2,1,0:T(8,128)S(1)}, f32[8,128]{1,0:T(8,128)S(1)}) custom-call(s32[4]{0:T(128)S(1)} %copy-done.1, s32[4]{0:T(128)S(1)} %copy-done.2, s32[4]{0:T(128)S(1)} %copy-done.3, f32[128,2048]{1,0:T(8,128)S(1)} %copy-done), custom_call_target="tpu_custom_call" | custom-call | tf_op jit(solution)/shard_map/exchange/pallas_call | solution.py:263
  51.6 2.7 %margin.1 = f32[4,128,2048]{2,1,0:T(8,128)} custom-call(f32[4,16,128,128]{3,2,1,0:T(8,128)S(1)} %get-tuple-element.8.lifted_ref, f32[4,16,128,128]{3,2,1,0:T(8,128)S(1)} %get-tuple-element.9.running_ref, f32[8,128]{1,0:T(8,128)S(1)} %get-tuple-element.10.before_ref), custom_call_target="tpu_custom_call" | custom-call | tf_op jit(solution)/shard_map/margin/pallas_call | solution.py:287
Async XLA Ops:
  0.0 1.2 %copy-start = (f32[128,2048]{1,0:T(8,128)S(1)}, f32[128,2048]{1,0:T(8,128)}, u32[]{:S(2)}) copy-start(f32[128,2048]{1,0:T(8,128)} %surface_hbm.1) | copy-start | bytes 3145732
  1.2 0.7 %copy-start.1 = (s32[4]{0:T(128)S(1)}, s32[4]{0:T(128)}, u32[]{:S(2)}) copy-start(s32[4]{0:T(128)} %bearing_ref.1) | copy-start | bytes 52
  1.9 0.7 %copy-start.2 = (s32[4]{0:T(128)S(1)}, s32[4]{0:T(128)}, u32[]{:S(2)}) copy-start(s32[4]{0:T(128)} %shift_ref.1) | copy-start | bytes 52
  2.5 0.7 %copy-start.3 = (s32[4]{0:T(128)S(1)}, s32[4]{0:T(128)}, u32[]{:S(2)}) copy-start(s32[4]{0:T(128)} %camera_ref.1) | copy-start | bytes 52

commit v2 on v1

--- a/solution.py
+++ b/solution.py
@@ -38,7 +38,7 @@
 def exchange_kernel(
     bearing_ref, shift_ref, camera_ref, surface_hbm,
     lifted_ref, running_ref, before_ref,
-    surf, above, below, edge, peaks, edge_peaks, message, inbox,
+    surf, above, below, edge, peaks, edge_peaks, message, inbox, turned, edge_lift,
     load_sem, up_send, up_recv, down_send, down_recv, peak_send, peak_recv,
 ):
     rows, cols = surface_hbm.shape
@@ -102,7 +102,7 @@
     def _():
         to_above().start()
 
-    def stencil(read, row):
+    def stencil(read, row, e=None):
         top = [None] * AZIMUTHS
         for c in range(chunks):
             col = first + float(c * LANES)
@@ -112,6 +112,8 @@
                     acc = acc + weights[k][j] * read(c, k, j)
                 acc = acc + rise[k] * col
                 lifted_ref[k, c, pl.ds(row, SUB), :] = acc
+                if e is not None:
+                    edge_lift[c, pl.ds((2 * k + e) * SUB, SUB), :] = acc
                 top[k] = acc if c == 0 else jnp.maximum(top[k], acc)
         return top
 
@@ -135,6 +137,55 @@
         (SUB - AZIMUTHS, rows), -jnp.inf, jnp.float32
     )
     before_ref[...] = jnp.full(before_ref.shape, -jnp.inf, jnp.float32)
+
+    group = LANES // SUB
+    sub = lax.broadcasted_iota(jnp.int32, (SUB, LANES), 0)
+    span = max(n for n in (1, 2, 4) if chunks % n == 0)
+    pair = 2 if chunks % 2 == 0 else 1
+
+    def scan_blocks(blocks, carries):
+        for slot, (load_block, _, _) in enumerate(blocks):
+            turned[slot] = load_block().T
+        for slot, (_, _, chain) in enumerate(blocks):
+            run = []
+            for v in range(group):
+                x = turned[slot, pl.ds(v, SUB, stride=group), :]
+                run.append(x if v == 0 else jnp.maximum(run[-1], x))
+            total = run[-1]
+            for step in (1, 2, 4):
+                moved = pltpu.roll(total, step, axis=0)
+                total = jnp.maximum(total, jnp.where(sub >= step, moved, total))
+            carry = carries[chain]
+            shifted = jnp.where(sub >= 1, pltpu.roll(total, 1, axis=0), carry)
+            offset = jnp.maximum(shifted, carry)
+            last = jnp.broadcast_to(total[SUB - 1 :, :], (SUB, LANES))
+            carries[chain] = jnp.maximum(carry, last)
+            for v in range(group):
+                turned[slot, pl.ds(v, SUB, stride=group), :] = jnp.maximum(run[v], offset)
+        for slot, (_, store_block, _) in enumerate(blocks):
+            store_block(turned[slot].T)
+        return carries
+
+    def inner_scan(q, carries):
+        def load(k, c):
+            return lambda: lifted_ref[k, q * pair + c]
+
+        def store(k, c):
+            def put(x):
+                running_ref[k, q * pair + c] = x
+
+            return put
+
+        blocks = [
+            (load(k, c), store(k, c), k) for c in range(pair) for k in range(AZIMUTHS)
+        ]
+        return tuple(scan_blocks(blocks, list(carries)))
+
+    lax.fori_loop(0, chunks // pair, inner_scan, (lowest,) * AZIMUTHS)
+    for c in range(chunks):
+        edge_lift[c, pl.ds(2 * AZIMUTHS * SUB, LANES - 2 * AZIMUTHS * SUB), :] = jnp.zeros(
+            (LANES - 2 * AZIMUTHS * SUB, LANES), jnp.float32
+        )
 
     @pl.when(ty == 0)
     def _():
@@ -163,6 +214,7 @@
         top = stencil(
             lambda c, k, j: edge[e, c, pl.ds(SUB + shift_ref[k] + (j - 1), SUB), :],
             e * (rows - SUB),
+            e,
         )
         for k in range(AZIMUTHS):
             edge_peaks[pl.ds((2 * k + e) * SUB, SUB), :] = top[k]
@@ -190,23 +242,25 @@
         def _():
             to_right(i).start()
 
-    def scan(q, _):
-        k = q // tiles
-        row = pl.multiple_of((q % tiles) * SUB, SUB)
-        carry = None
-        for c in range(chunks):
-            x = lifted_ref[k, c, pl.ds(row, SUB), :]
-            step = 1
-            while step < LANES:
-                rolled = pltpu.roll(x, step, axis=1)
-                x = jnp.maximum(x, jnp.where(lane >= step, rolled, x))
-                step *= 2
-            last = jnp.broadcast_to(x[:, LANES - 1 :], (SUB, LANES))
-            running_ref[k, c, pl.ds(row, SUB), :] = x if c == 0 else jnp.maximum(x, carry)
-            carry = last if c == 0 else jnp.maximum(carry, last)
-        return 0
-
-    lax.fori_loop(0, AZIMUTHS * tiles, scan, 0)
+    def edge_scan(q, carry):
+        def load(c):
+            return lambda: edge_lift[q * span + c]
+
+        def store(c):
+            def put(x):
+                for k in range(AZIMUTHS):
+                    at = 2 * k * SUB
+                    running_ref[k, q * span + c, pl.ds(0, SUB), :] = x[at : at + SUB]
+                    running_ref[k, q * span + c, pl.ds(rows - SUB, SUB), :] = (
+                        x[at + SUB : at + 2 * SUB]
+                    )
+
+            return put
+
+        blocks = [(load(c), store(c), 0) for c in range(span)]
+        return tuple(scan_blocks(blocks, [carry[0]]))
+
+    lax.fori_loop(0, chunks // span, edge_scan, (lowest,))
 
     for i in range(nx):
 
@@ -274,13 +328,15 @@
             pltpu.VMEM((LANES, LANES), f32),
             pltpu.VMEM((SUB, rows), f32),
             pltpu.VMEM((nx, SUB, rows), f32),
+            pltpu.VMEM((2 * AZIMUTHS, LANES, LANES), f32),
+            pltpu.VMEM((chunks, LANES, LANES), f32),
             dma((chunks,)),
             dma, dma, dma, dma,
             dma((nx,)),
             dma((nx,)),
         ],
         compiler_params=pltpu.CompilerParams(
-            collective_id=0, has_side_effects=True, vmem_limit_bytes=24 * 2**20
+            collective_id=0, has_side_effects=True, vmem_limit_bytes=56 * 2**20 - 2**17
         ),
         name="exchange",
     )(bearing_index, stencil_displacements, camera_altitude_class, surface_levels)

time: 54.5 us -> 17.4 us (0.32)
  Pallas kernels: 51.1 us -> 17.2 us
  local copies, waits for them, and re-layouts: 3.19 us -> 0 us
    pallas_call x1, Pallas kernels: 48.4 us -> 14.5 us  [on_device(): pl.pallas_call(exchange_kernel, out_shape=(pltpu.VMEM(block, f32), pltpu....]
    unnamed x8 -> x0, local copies, waits for them, and re-layouts: 3.19 us -> none
where the time goes in v2:
time: 17.4 us; the launch traced here: 17.3 us
  Pallas kernels  17.2 us (99%)
    pallas_call x1, Pallas kernels, on_device(): pl.pallas_call(exchange_kernel, out_shape=(pltpu.VMEM(block, f32), pltpu....  14.5 us
    pallas_call x1, Pallas kernels, on_device(): pl.pallas_call(margin_kernel, out_shape=jax.ShapeDtypeStruct((AZIMUTHS, r...  2.72 us

profile of v2, /device:TPU:0, one launch (start us, length us, event | category | flops | bytes accessed | tf_op | source)
XLA Modules:
  0.0 17.3 jit_solution(10038421659924488649)
XLA Ops:
  0.0 14.5 %exchange.1 = (f32[4,16,128,128]{3,2,1,0:T(8,128)S(1)}, f32[4,16,128,128]{3,2,1,0:T(8,128)S(1)}, f32[8,128]{1,0:T(8,128)S(1)}) custom-call(s32[4]{0:T(128)} %bearing_ref.1, s32[4]{0:T(128)} %shift_ref.1, s32[4]{0:T(128)} %camera_ref.1, f32[128,2048]{1,0:T(8,128)} %surface_hbm.1), custom_call_target="tpu_custom_call" | custom-call | tf_op jit(solution)/shard_map/exchange/pallas_call | solution.py:317
  14.5 2.7 %margin.1 = f32[4,128,2048]{2,1,0:T(8,128)} custom-call(f32[4,16,128,128]{3,2,1,0:T(8,128)S(1)} %get-tuple-element.8.lifted_ref, f32[4,16,128,128]{3,2,1,0:T(8,128)S(1)} %get-tuple-element.9.running_ref, f32[8,128]{1,0:T(8,128)S(1)} %get-tuple-element.10.before_ref), custom_call_target="tpu_custom_call" | custom-call | tf_op jit(solution)/shard_map/margin/pallas_call | solution.py:343

commit v3 on v2

--- a/solution.py
+++ b/solution.py
@@ -79,9 +79,6 @@
 
     for c in range(chunks):
         load(c).wait()
-    sends = jnp.where(ty > 0, 1, 0) + jnp.where(ty < ny - 1, 1, 0) + (nx - 1 - tx)
-    pl.semaphore_wait(barrier, sends)
-
     def to_above():
         return pltpu.make_async_remote_copy(
             surf.at[:, pl.ds(0, SUB), :], below, up_send, up_recv,
@@ -93,14 +90,6 @@
             surf.at[:, pl.ds(rows - SUB, SUB), :], above, down_send, down_recv,
             device_id={"ty": ty + 1}, device_id_type=MESH,
         )
-
-    @pl.when(ty < ny - 1)
-    def _():
-        to_below().start()
-
-    @pl.when(ty > 0)
-    def _():
-        to_above().start()
 
     def stencil(read, row, e=None):
         top = [None] * AZIMUTHS
@@ -130,7 +119,20 @@
     for k in range(AZIMUTHS):
         peaks[k, pl.ds(0, SUB), :] = lowest
         peaks[k, pl.ds(rows - SUB, SUB), :] = lowest
-    lax.fori_loop(1, tiles - 1, inner, 0)
+    early = 1 + (tiles - 2) * (nx - tx) // nx
+    lax.fori_loop(1, early, inner, 0)
+    sends = jnp.where(ty > 0, 1, 0) + jnp.where(ty < ny - 1, 1, 0) + (nx - 1 - tx)
+    pl.semaphore_wait(barrier, sends)
+
+    @pl.when(ty < ny - 1)
+    def _():
+        to_below().start()
+
+    @pl.when(ty > 0)
+    def _():
+        to_above().start()
+
+    lax.fori_loop(early, tiles - 1, inner, 0)
     for k in range(AZIMUTHS):
         message[pl.ds(k, 1), :] = jnp.max(peaks[k].T, axis=0, keepdims=True)
     message[pl.ds(AZIMUTHS, SUB - AZIMUTHS), :] = jnp.full(

time: 17.4 us -> 16.2 us (0.931)
  Pallas kernels: 17.2 us -> 16.1 us
    pallas_call x1, Pallas kernels: 14.5 us -> 13.3 us  [on_device(): pl.pallas_call(exchange_kernel, out_shape=(pltpu.VMEM(block, f32), pltpu....]
where the time goes in v3:
time: 16.2 us; the launch traced here: 16.1 us
  Pallas kernels  16.1 us (99%)
    pallas_call x1, Pallas kernels, on_device(): pl.pallas_call(exchange_kernel, out_shape=(pltpu.VMEM(block, f32), pltpu....  13.3 us
    pallas_call x1, Pallas kernels, on_device(): pl.pallas_call(margin_kernel, out_shape=jax.ShapeDtypeStruct((AZIMUTHS, r...  2.72 us

profile of v3, /device:TPU:0, one launch (start us, length us, event | category | flops | bytes accessed | tf_op | source)
XLA Modules:
  0.0 16.1 jit_solution(4588117905115092462)
XLA Ops:
  0.0 13.3 %exchange.1 = (f32[4,16,128,128]{3,2,1,0:T(8,128)S(1)}, f32[4,16,128,128]{3,2,1,0:T(8,128)S(1)}, f32[8,128]{1,0:T(8,128)S(1)}) custom-call(s32[4]{0:T(128)} %bearing_ref.1, s32[4]{0:T(128)} %shift_ref.1, s32[4]{0:T(128)} %camera_ref.1, f32[128,2048]{1,0:T(8,128)} %surface_hbm.1), custom_call_target="tpu_custom_call" | custom-call | tf_op jit(solution)/shard_map/exchange/pallas_call | solution.py:319
  13.4 2.7 %margin.1 = f32[4,128,2048]{2,1,0:T(8,128)} custom-call(f32[4,16,128,128]{3,2,1,0:T(8,128)S(1)} %get-tuple-element.8.lifted_ref, f32[4,16,128,128]{3,2,1,0:T(8,128)S(1)} %get-tuple-element.9.running_ref, f32[8,128]{1,0:T(8,128)S(1)} %get-tuple-element.10.before_ref), custom_call_target="tpu_custom_call" | custom-call | tf_op jit(solution)/shard_map/margin/pallas_call | solution.py:345
